TPU v7x, 32 devices: a whole 2x2x4 slice. The times are simulated.
32 devices in a mesh: seq: 8 (over z, y), head: 4 (over x, core).
Axes of the slice: x: 2, y: 2, z: 4, core: 2. Of those that a mesh axis runs over, the one named last changes fastest.
Arguments:
- queries: bfloat16 [4096, 2048], P('seq', 'head'), may hold values from -6 to 6
- key_vectors: bfloat16 [4096, 2048], P('seq', 'head'), may hold values from -6 to 6
- value_vectors: bfloat16 [4096, 2048], P('seq', 'head'), may hold values from -6 to 6
- gate_input: bfloat16 [4096, 2048], P('seq', 'head'), may hold values from -6 to 6
- out_weight: bfloat16 [2048, 4096], P('seq', 'head'), may hold values from -0.125 to 0.125
Outputs:
- layer_output: bfloat16 [4096, 4096], P('seq', 'head')
All inputs are finite; a program needn't handle non-finite values.
Results may differ from a plain program's by a relative error of at most 0.0057.
Values may be sent and summed in bfloat16 or wider, within the bound.
A program may use at most 64 MiB of HBM per device.

v0:
```python
import jax
import jax.numpy as jnp
from jax import lax
from jax.sharding import PartitionSpec as P

HD = 128


def carried_in(shard, axis, combine, identity):
    count, position = (lax.axis_size(axis), lax.axis_index(axis))
    everything = lax.all_gather(shard, axis)
    start = jnp.broadcast_to(jnp.asarray(identity, shard.dtype), shard.shape)

    def turn(k, before):
        reached = k < position
        new = combine(before, everything[k])
        return jnp.where(reached, new, before)

    return lax.fori_loop(0, count, turn, start)


def add_states(earlier, later):
    return earlier + later


def carried(own_state):
    return carried_in(own_state, "seq", add_states, jnp.zeros_like(own_state))


def in_shard(qhead, khead, vhead, scale):
    rows = qhead.shape[0]
    step = min(rows, 512)
    scores = jnp.einsum("thd,shd->hts", qhead, khead, preferred_element_type=jnp.float32) * scale
    rowpos = 0 + lax.broadcasted_iota(jnp.int32, (step, step), 0)
    colpos = lax.broadcasted_iota(jnp.int32, (step, step), 1)
    scores = jnp.where((colpos <= rowpos)[None, :, :], scores, 0.0).astype(jnp.bfloat16)
    pieces = jnp.einsum("hts,she->the", scores, vhead, preferred_element_type=jnp.float32)
    return pieces


def per_device(queries, key_vectors, value_vectors, gate_input, out_weight):
    rows, width = queries.shape
    heads = width // HD
    scale = HD ** (-0.5)
    qhead = queries.reshape(rows, heads, HD)
    khead = key_vectors.reshape(rows, heads, HD)
    vhead = value_vectors.reshape(rows, heads, HD)
    own_state = jnp.einsum("thd,the->hde", khead, vhead, preferred_element_type=jnp.float32)
    local = in_shard(qhead, khead, vhead, scale)
    prefix = carried(own_state)
    inter = (
        jnp.einsum(
            "thd,hde->the", qhead, prefix.astype(jnp.bfloat16), preferred_element_type=jnp.float32
        )
        * scale
    )
    attn = (local + inter).reshape(rows, width)
    squares = jnp.sum(attn * attn, axis=1)
    hidden = (attn * jax.nn.silu(gate_input.astype(jnp.float32))).astype(jnp.bfloat16)
    total = lax.psum(squares, "head")
    features = lax.all_gather(hidden, "head", axis=1, tiled=True)
    full_block = lax.all_gather(out_weight, "seq", axis=0, tiled=True)
    projected = jnp.dot(features, full_block, preferred_element_type=jnp.float32)
    mean_square = total / features.shape[1]
    return (projected * lax.rsqrt(mean_square + 1e-06)[:, None]).astype(jnp.bfloat16)


def solution(mesh):
    placed = (
        P("seq", "head"),
        P("seq", "head"),
        P("seq", "head"),
        P("seq", "head"),
        P("seq", "head"),
    )
    return jax.shard_map(
        per_device, mesh=mesh, in_specs=placed, out_specs=P("seq", "head"), check_vma=False
    )
```

profile of v0, /device:TPU:0, one launch (start us, length us, event | category | flops | bytes accessed | tf_op | source)
XLA Modules:
  0.0 184.2 jit_solution(1914398323355310470)
XLA Ops:
  6.5 1.3 copy.19
  7.9 2.0 %fusion.10 = f32[4,128,128]{2,1,0:T(8,128)} fusion(bf16[512,4,128]{0,2,1:T(8,128)(2,1)S(1)} %bitcast.47, bf16[512,512]{1,0:T(8,128)(2,1)} %param.9), kind=kOutput, calls=%fused_computation.18 | convolution fusion | flops 67108864 | bytes 1310720 | tf_op jit(solution)/shard_map/thd,the->hde/dot_general | solution.py:48
  9.9 0.0 all-gather.5.cloned.1.call-start
  10.0 0.1 iota_compare_fusion
  10.1 51.8 %all-gather.9.cloned.1.call-done = f32[32,128,128]{2,1,0:T(8,128)} async-done(((f32[4,128,128]{2,1,0:T(8,128)}), f32[32,128,128]{2,1,0:T(8,128)}) %all-gather.9.cloned.1.call-update) | async-done | bytes 2097168 | tf_op jit(solution)/shard_map/all_gather | solution.py:11
  61.9 8.5 %while.14 = (s32[]{:T(128)}, f32[4,128,128]{2,1,0:T(8,128)S(1)}, s32[]{:T(128)}, f32[8,4,128,128]{3,2,1,0:T(8,128)}, s32[]{:T(128)}, /*index=5*/s32[]{:T(128)}) while((s32[]{:T(128)}, f32[4,128,128]{2,1,0:T(8,128)S(1)}, s32[]{:T(128)}, f32[8,4,128,128]{3,2,1,0:T(8,128)}, s32[]{:T(128)}, /*index=5*/s32[]{:T(128)}) %tuple.42), condition=%wide.region_1.2_spmd.clone, body=%wide.region_0.1_spmd.clone.sunk | while | flops 196612 | bytes 786525 | solution.py:19
  61.9 1.0 add_select_fusion.2
  62.9 1.0 add_select_fusion.2
  64.0 1.0 add_select_fusion.2
  65.1 1.0 add_select_fusion.2
  66.1 1.0 add_select_fusion.2
  67.2 1.0 add_select_fusion.2
  68.3 1.0 add_select_fusion.2
  69.3 1.0 add_select_fusion.2
  70.4 0.3 fusion.3
  70.7 2.4 %multiply_reduce_fusion = (f32[512]{0:T(512)S(1)}, f32[512,4,128]{0,2,1:T(8,128)S(1)}) fusion(f32[512,4,128]{0,2,1:T(8,128)S(1)} %fusion.3, bf16[512,4,128]{0,2,1:T(8,128)(2,1)S(1)} %bitcast.48, pred[512,512]{1,0:T(8,128)(4,1)S(1)} %iota_compare_fusion, bf16[512,512]{1,0:T(8,128)(2,1)} %param.9, bf16[512,512]{1,0:T(8,128)(2,1)S(1)} %copy-done), kind=kOutput, calls=%fused_computation.14 | convolution fusion | flops 540802560 | bytes 3934208 | tf_op jit(solution)/shard_map/hts,she->the/dot_general | solution.py:37
  73.2 0.3 copy.17
  73.5 0.7 copy-done.1
  74.2 1.1 fusion.8
  75.4 0.7 all-gather.7.cloned.1.call-update
  76.1 5.7 %psum.7 = f32[512]{0:T(512)S(1)} all-reduce(f32[512]{0:T(512)S(1)} %get-tuple-element.108), channel_id=1, replica_groups=mesh['seq'=8,'head'=4] {'head'}, use_global_device_ids=true, to_apply=%region_3.4 | all-reduce | flops 512 | bytes 4096 | tf_op jit(solution)/shard_map/psum | solution.py:60
  81.8 14.8 %all-gather.5.cloned.1.call-done = bf16[512,2048]{1,0:T(8,128)(2,1)} async-done(((bf16[512,512]{1,0:T(8,128)(2,1)}), bf16[512,2048]{1,0:T(8,128)(2,1)}) %all-gather.5.cloned.1.call-update) | async-done | bytes 2097168 | tf_op jit(solution)/shard_map/all_gather | solution.py:61
  96.6 75.0 %all-gather.7.cloned.1.call-done = bf16[2048,1024]{1,0:T(8,128)(2,1)} async-done(((bf16[256,1024]{1,0:T(8,128)(2,1)}), bf16[2048,1024]{1,0:T(8,128)(2,1)}) %all-gather.7.cloned.1.call-update) | async-done | bytes 4194320 | tf_op jit(solution)/shard_map/all_gather | solution.py:62
  171.6 6.1 %multiply_convert_fusion = bf16[512,1024]{1,0:T(8,128)(2,1)} fusion(bf16[512,2048]{1,0:T(8,128)(2,1)} %all-gather.5.cloned.1.call-done, bf16[2048,1024]{1,0:T(8,128)(2,1)} %all-gather.7.cloned.1.call-done, f32[512]{0:T(512)S(1)} %add_rsqrt_fusion), kind=kOutput, calls=%fused_computation.2 | convolution fusion | flops 2148532224 | bytes 7342080 | tf_op jit(solution)/shard_map/dot_general | solution.py:63
  (9 shorter events, 0.1 us)
Async XLA Ops:
  6.5 63.9 %copy-start = (bf16[512,512]{1,0:T(8,128)(2,1)S(1)}, bf16[512,512]{1,0:T(8,128)(2,1)}, u32[]{:S(2)}) copy-start(bf16[512,512]{1,0:T(8,128)(2,1)} %param.7) | copy-start | bytes 1572868
  6.5 55.3 %all-gather.9.cloned.1.call-start = ((), (), s32[]{:S(2)}) async-start(), calls=%async_computation.2 | async-start | bytes 2359296 | tf_op jit(solution)/shard_map/all_gather | solution.py:11
  9.9 86.7 %all-gather.5.cloned.1.call-start = ((), (), s32[]{:S(2)}) async-start(), calls=%async_computation | async-start | bytes 2621440 | tf_op jit(solution)/shard_map/all_gather | solution.py:61
  73.2 1.0 copy-start.1
  75.3 96.2 %all-gather.7.cloned.1.call-start = ((), (), s32[]{:S(2)}) async-start(), calls=%async_computation.1 | async-start | bytes 4718592 | tf_op jit(solution)/shard_map/all_gather | solution.py:62
Sparse Core Ops, SparseCore 0:
  10.0 51.7 all-gather.8
  75.5 21.0 all-gather.4
  98.7 72.7 all-gather.6
where the time goes:
time: 185 us; the launch traced here: 184 us
  waiting for transfers between devices  142 us (77%)
  between operations  13.2 us (7%)
  matrix products  10.9 us (6%)
  other arithmetic  9.53 us (5%)
  blocking collectives  5.67 us (3%)
  local copies, waits for them, and re-layouts  2.34 us (1%)
    all_gather x1, waiting for transfers between devices, per_device(): full_block = lax.all_gather(out_weight, 'seq', axis=0, tiled=True)  75 us
    all_gather x1, waiting for transfers between devices, carried_in(): everything = lax.all_gather(shard, axis)  51.8 us
    all_gather x1, waiting for transfers between devices, per_device(): features = lax.all_gather(hidden, 'head', axis=1, tiled=True)  14.8 us
    select_n x8, other arithmetic, turn(): return jnp.where(reached, new, before)  8.32 us
    dot_general x1, matrix products, per_device(): jnp.dot(features, full_block, preferred_element_type=jnp.float32)  6.12 us
    psum x1, blocking collectives, per_device(): total = lax.psum(squares, 'head')  5.67 us
  transfers between devices with their start and end apart: 3, of which 3 were waited for; matrix products, arithmetic and copies ran while one was open for 0% of the time, Pallas kernels for 0%

commit v1 on v0

--- a/solution.py
+++ b/solution.py
@@ -59,7 +59,12 @@
     hidden = (attn * jax.nn.silu(gate_input.astype(jnp.float32))).astype(jnp.bfloat16)
     total = lax.psum(squares, "head")
     features = lax.all_gather(hidden, "head", axis=1, tiled=True)
-    full_block = lax.all_gather(out_weight, "seq", axis=0, tiled=True)
+    ring = [out_weight]
+    for hop in range(7):
+        ring.append(lax.ppermute(ring[-1], "seq", [(dev, (dev + 1) % 8) for dev in range(8)]))
+    full_block = jnp.roll(
+        jnp.concatenate(ring[::-1], axis=0), (lax.axis_index("seq") + 1) * ring[0].shape[0], axis=0
+    )
     projected = jnp.dot(features, full_block, preferred_element_type=jnp.float32)
     mean_square = total / features.shape[1]
     return (projected * lax.rsqrt(mean_square + 1e-06)[:, None]).astype(jnp.bfloat16)

time: 185 us -> 163 us (0.88)
  waiting for transfers between devices: 142 us -> 98.3 us
  local copies, waits for them, and re-layouts: 2.34 us -> 15 us
  starting transfers between devices: 0.09 us -> 4.13 us
  matrix products: 10.9 us -> 13.2 us
  other arithmetic: 9.53 us -> 11.4 us
    ppermute x0 -> x7, waiting for transfers between devices: none -> 98.3 us  [per_device(): lax.ppermute(ring[-1], 'seq', [(dev, (dev + 1) % 8) for dev in range(8)])]
    all_gather x1 -> x0, waiting for transfers between devices: 75 us -> none  [per_device(): full_block = lax.all_gather(out_weight, 'seq', axis=0, tiled=True)]
    all_gather x1, waiting for transfers between devices: 51.8 us -> 0.01 us  [carried_in(): everything = lax.all_gather(shard, axis)]
    all_gather x1, waiting for transfers between devices: 14.8 us -> 0.01 us  [per_device(): features = lax.all_gather(hidden, 'head', axis=1, tiled=True)]
    unnamed x4 -> x31, local copies, waits for them, and re-layouts: 0.7 us -> 12.1 us
    ppermute x0 -> x7, starting transfers between devices: none -> 4.09 us  [per_device(): lax.ppermute(ring[-1], 'seq', [(dev, (dev + 1) % 8) for dev in range(8)])]
  transfers between devices with their start and end apart: 3 -> 9, of which waited for: 3 -> 6; matrix products, arithmetic and copies ran while one was open for 0% -> 17% of each run, Pallas kernels for 0% -> 0%
where the time goes in v1:
time: 163 us; the launch traced here: 162 us
  waiting for transfers between devices  98.3 us (60%)
  local copies, waits for them, and re-layouts  15 us (9%)
  between operations  13.6 us (8%)
  matrix products  13.2 us (8%)
  other arithmetic  11.4 us (7%)
  blocking collectives  6.39 us (4%)
  starting transfers between devices  4.13 us (3%)
    ppermute x7, waiting for transfers between devices, per_device(): lax.ppermute(ring[-1], 'seq', [(dev, (dev + 1) % 8) for dev in range(8)])  98.3 us
    unnamed x31, local copies, waits for them, and re-layouts  12.1 us
    select_n x8, other arithmetic, turn(): return jnp.where(reached, new, before)  8.32 us
    psum x1, blocking collectives, per_device(): total = lax.psum(squares, 'head')  6.39 us
    dot_general x1, matrix products, per_device(): jnp.dot(features, full_block, preferred_element_type=jnp.float32)  6.13 us
    ppermute x7, starting transfers between devices, per_device(): lax.ppermute(ring[-1], 'seq', [(dev, (dev + 1) % 8) for dev in range(8)])  4.09 us
    dot_general x1, matrix products, in_shard(): jnp.einsum('hts,she->the', scores, vhead, preferred_element_type=jnp.floa...  3.69 us
  transfers between devices with their start and end apart: 9, of which 6 were waited for; matrix products, arithmetic and copies ran while one was open for 17% of the time, Pallas kernels for 0%

profile of v1, /device:TPU:0, one launch (start us, length us, event | category | flops | bytes accessed | tf_op | source)
XLA Modules:
  0.0 162.2 jit_solution(7619510253483718318)
XLA Ops:
  6.5 1.3 copy.19
  7.9 2.0 %fusion.14 = f32[4,128,128]{2,1,0:T(8,128)} fusion(bf16[512,4,128]{0,2,1:T(8,128)(2,1)S(1)} %bitcast.46, bf16[512,512]{1,0:T(8,128)(2,1)} %param.9), kind=kOutput, calls=%fused_computation.20 | convolution fusion | flops 67108864 | bytes 1310720 | tf_op jit(solution)/shard_map/thd,the->hde/dot_general | solution.py:48
  10.0 3.0 %collective-permute-start = (bf16[256,1024]{1,0:T(8,128)(2,1)}, bf16[256,1024]{1,0:T(8,128)(2,1)S(1)}, u32[]{:S(2)}, u32[]{:S(2)}) collective-permute-start(bf16[256,1024]{1,0:T(8,128)(2,1)} %param.11), channel_id=1, source_target_pairs={{0,4},{4,8},{8,12},{12,16},{16,20},{20,24},{24,28},{28,0},{1,5},{5... | collective-permute-start | bytes 1572872 | tf_op jit(solution)/shard_map/ppermute | solution.py:64
  13.0 17.8 %collective-permute-done = bf16[256,1024]{1,0:T(8,128)(2,1)S(1)} collective-permute-done((bf16[256,1024]{1,0:T(8,128)(2,1)}, bf16[256,1024]{1,0:T(8,128)(2,1)S(1)}, u32[]{:S(2)}, u32[]{:S(2)}) %collective-permute-start) | collective-permute-done | bytes 524320 | tf_op jit(solution)/shard_map/ppermute | solution.py:64
  30.9 17.2 %collective-permute-done.1 = bf16[256,1024]{1,0:T(8,128)(2,1)S(1)} collective-permute-done((bf16[256,1024]{1,0:T(8,128)(2,1)S(1)}, bf16[256,1024]{1,0:T(8,128)(2,1)S(1)}, u32[]{:S(2)}, u32[]{:S(2)}) %collective-permute-start.1) | collective-permute-done | bytes 524320 | tf_op jit(solution)/shard_map/ppermute | solution.py:64
  48.1 23.5 %collective-permute-done.2 = bf16[256,1024]{1,0:T(8,128)(2,1)S(1)} collective-permute-done((bf16[256,1024]{1,0:T(8,128)(2,1)S(1)}, bf16[256,1024]{1,0:T(8,128)(2,1)S(1)}, u32[]{:S(2)}, u32[]{:S(2)}) %collective-permute-start.2) | collective-permute-done | bytes 524320 | tf_op jit(solution)/shard_map/ppermute | solution.py:64
  72.5 15.8 %collective-permute-done.3 = bf16[256,1024]{1,0:T(8,128)(2,1)S(1)} collective-permute-done((bf16[256,1024]{1,0:T(8,128)(2,1)S(1)}, bf16[256,1024]{1,0:T(8,128)(2,1)S(1)}, u32[]{:S(2)}, u32[]{:S(2)}) %collective-permute-start.3) | collective-permute-done | bytes 524320 | tf_op jit(solution)/shard_map/ppermute | solution.py:64
  89.2 15.1 %collective-permute-done.4 = bf16[256,1024]{1,0:T(8,128)(2,1)} collective-permute-done((bf16[256,1024]{1,0:T(8,128)(2,1)S(1)}, bf16[256,1024]{1,0:T(8,128)(2,1)}, u32[]{:S(2)}, u32[]{:S(2)}) %collective-permute-start.4) | collective-permute-done | bytes 524320 | tf_op jit(solution)/shard_map/ppermute | solution.py:64
  104.3 8.5 %while.14 = (s32[]{:T(128)}, f32[4,128,128]{2,1,0:T(8,128)S(1)}, s32[]{:T(128)}, f32[8,4,128,128]{3,2,1,0:T(8,128)}, s32[]{:T(128)}, /*index=5*/s32[]{:T(128)}) while((s32[]{:T(128)}, f32[4,128,128]{2,1,0:T(8,128)S(1)}, s32[]{:T(128)}, f32[8,4,128,128]{3,2,1,0:T(8,128)}, s32[]{:T(128)}, /*index=5*/s32[]{:T(128)}) %tuple.40), condition=%wide.region_1.2_spmd.clone, body=%wide.region_0.1_spmd.clone.sunk | while | flops 196612 | bytes 786525 | solution.py:19
  112.8 1.3 fusion.7
  114.2 3.7 %multiply_reduce_fusion = (f32[512]{0:T(512)S(1)}, f32[512,4,128]{0,2,1:T(8,128)}) fusion(f32[512,4,128]{0,2,1:T(8,128)} %fusion.7, bf16[512,4,128]{0,2,1:T(8,128)(2,1)S(1)} %bitcast.47, pred[512,512]{1,0:T(8,128)(4,1)} %iota_compare_fusion, bf16[512,512]{1,0:T(8,128)(2,1)S(1)} %copy-done.6, bf16[512,512]{1,0:T(8,128)(2,1)S(1)} %copy-done), kind=kOutput, calls=%fused_computation.16 | convolution fusion | flops 540802560 | bytes 3934208 | tf_op jit(solution)/shard_map/hts,she->the/dot_general | solution.py:37
  117.9 1.6 copy.17
  119.4 2.2 %fusion.12 = bf16[512,512]{1,0:T(8,128)(2,1)} fusion(f32[512,512]{1,0:T(8,128)S(1)} %copy.17, bf16[512,512]{1,0:T(8,128)(2,1)} %param.10), kind=kLoop, calls=%fused_computation.18 | loop fusion | flops 1835008 | bytes 2097152 | tf_op jit(solution)/shard_map/convert_element_type | solution.py:59
  121.7 6.4 %psum.7 = f32[512]{0:T(512)S(1)} all-reduce(f32[512]{0:T(512)S(1)} %get-tuple-element.108), channel_id=1, replica_groups=mesh['seq'=8,'head'=4] {'head'}, use_global_device_ids=true, to_apply=%region_3.4 | all-reduce | flops 512 | bytes 4096 | tf_op jit(solution)/shard_map/psum | solution.py:60
  128.1 8.9 %collective-permute-done.6 = bf16[256,1024]{1,0:T(8,128)(2,1)} collective-permute-done((bf16[256,1024]{1,0:T(8,128)(2,1)}, bf16[256,1024]{1,0:T(8,128)(2,1)}, u32[]{:S(2)}, u32[]{:S(2)}) %collective-permute-start.6) | collective-permute-done | bytes 524320 | tf_op jit(solution)/shard_map/ppermute | solution.py:64
  138.1 1.1 constant_dynamic-update-slice_fusion.14
  139.2 1.1 constant_dynamic-update-slice_fusion.13
  140.2 1.1 constant_dynamic-update-slice_fusion.12
  141.3 1.1 constant_dynamic-update-slice_fusion.11
  142.5 1.1 constant_dynamic-update-slice_fusion.7
  143.6 1.1 constant_dynamic-update-slice_fusion.6
  144.7 1.1 constant_dynamic-update-slice_fusion.5
  146.0 3.2 %copy-done.7 = bf16[4096,1024]{1,0:T(8,128)(2,1)} copy-done((bf16[4096,1024]{1,0:T(8,128)(2,1)}, bf16[4096,1024]{1,0:T(8,128)(2,1)S(1)}, u32[]{:S(2)}) %copy-start.7) | copy-done | bytes 8388632
  149.3 6.1 %multiply_convert_fusion = bf16[512,1024]{1,0:T(8,128)(2,1)} fusion(bf16[512,2048]{1,0:T(8,128)(2,1)} %all-gather.4.cloned.1.call-done, bf16[4096,1024]{1,0:T(8,128)(2,1)} %copy-done.7, s32[]{:T(128)S(6)} %select_n.40, f32[512]{0:T(512)S(1)} %add_rsqrt_fusion), kind=kOutput, calls=%fused_computation.4 | convolution fusion | flops 2148532224 | bytes 7342084 | tf_op jit(solution)/shard_map/dot_general | solution.py:68
  (48 shorter events, 11.7 us)
Async XLA Ops:
  6.5 106.3 %copy-start = (bf16[512,512]{1,0:T(8,128)(2,1)S(1)}, bf16[512,512]{1,0:T(8,128)(2,1)}, u32[]{:S(2)}) copy-start(bf16[512,512]{1,0:T(8,128)(2,1)} %param.7) | copy-start | bytes 1572868
  6.5 107.6 %copy-start.6 = (bf16[512,512]{1,0:T(8,128)(2,1)S(1)}, bf16[512,512]{1,0:T(8,128)(2,1)}, u32[]{:S(2)}) copy-start(bf16[512,512]{1,0:T(8,128)(2,1)} %param.9) | copy-start | bytes 1572868
  6.5 97.8 %all-gather.6.cloned.1.call-start = ((), (), s32[]{:S(2)}) async-start(), calls=%async_computation.1 | async-start | bytes 2359296 | tf_op jit(solution)/shard_map/all_gather | solution.py:11
  10.0 139.3 %all-gather.4.cloned.1.call-start = ((), (), s32[]{:S(2)}) async-start(), calls=%async_computation | async-start | bytes 2621440 | tf_op jit(solution)/shard_map/all_gather | solution.py:61
  10.0 20.9 %collective-permute-start = (bf16[256,1024]{1,0:T(8,128)(2,1)}, bf16[256,1024]{1,0:T(8,128)(2,1)S(1)}, u32[]{:S(2)}, u32[]{:S(2)}) collective-permute-start(bf16[256,1024]{1,0:T(8,128)(2,1)} %param.11), channel_id=1, source_target_pairs={{0,4},{4,8},{8,12},{12,16},{16,20},{20,24},{24,28},{28,0},{1,5},{5... | collective-permute-start | bytes 1572872 | tf_op jit(solution)/shard_map/ppermute | solution.py:64
  30.9 17.2 %collective-permute-start.1 = (bf16[256,1024]{1,0:T(8,128)(2,1)S(1)}, bf16[256,1024]{1,0:T(8,128)(2,1)S(1)}, u32[]{:S(2)}, u32[]{:S(2)}) collective-permute-start(bf16[256,1024]{1,0:T(8,128)(2,1)S(1)} %collective-permute-done), channel_id=1, source_target_pairs={{0,4},{4,8},{8,12},{12,16},{16,20},{20,24},{24,28},{28,0},{1,5},{5... | collective-permute-start | bytes 1572872 | tf_op jit(solution)/shard_map/ppermute | solution.py:64
  48.1 23.5 %collective-permute-start.2 = (bf16[256,1024]{1,0:T(8,128)(2,1)S(1)}, bf16[256,1024]{1,0:T(8,128)(2,1)S(1)}, u32[]{:S(2)}, u32[]{:S(2)}) collective-permute-start(bf16[256,1024]{1,0:T(8,128)(2,1)S(1)} %collective-permute-done.1), channel_id=1, source_target_pairs={{0,4},{4,8},{8,12},{12,16},{16,20},{20,24},{24,28},{28,0},{1,5},{5... | collective-permute-start | bytes 1572872 | tf_op jit(solution)/shard_map/ppermute | solution.py:64
  71.6 16.8 %copy-start.2 = (bf16[256,1024]{1,0:T(8,128)(2,1)}, bf16[256,1024]{1,0:T(8,128)(2,1)S(1)}, u32[]{:S(2)}) copy-start(bf16[256,1024]{1,0:T(8,128)(2,1)S(1)} %collective-permute-done.2) | copy-start | bytes 1572868
  71.6 16.8 %collective-permute-start.3 = (bf16[256,1024]{1,0:T(8,128)(2,1)S(1)}, bf16[256,1024]{1,0:T(8,128)(2,1)S(1)}, u32[]{:S(2)}, u32[]{:S(2)}) collective-permute-start(bf16[256,1024]{1,0:T(8,128)(2,1)S(1)} %collective-permute-done.2), channel_id=1, source_target_pairs={{0,4},{4,8},{8,12},{12,16},{16,20},{20,24},{24,28},{28,0},{1,5},{5... | collective-permute-start | bytes 1572872 | tf_op jit(solution)/shard_map/ppermute | solution.py:64
  88.3 24.5 %copy-start.4 = (bf16[256,1024]{1,0:T(8,128)(2,1)}, bf16[256,1024]{1,0:T(8,128)(2,1)S(1)}, u32[]{:S(2)}) copy-start(bf16[256,1024]{1,0:T(8,128)(2,1)S(1)} %collective-permute-done.3) | copy-start | bytes 1572868
  88.3 16.0 %collective-permute-start.4 = (bf16[256,1024]{1,0:T(8,128)(2,1)S(1)}, bf16[256,1024]{1,0:T(8,128)(2,1)}, u32[]{:S(2)}, u32[]{:S(2)}) collective-permute-start(bf16[256,1024]{1,0:T(8,128)(2,1)S(1)} %collective-permute-done.3), channel_id=1, source_target_pairs={{0,4},{4,8},{8,12},{12,16},{16,20},{20,24},{24,28},{28,0},{1,5},{5... | collective-permute-start | bytes 1572872 | tf_op jit(solution)/shard_map/ppermute | solution.py:64
  104.3 17.3 %collective-permute-start.5 = (bf16[256,1024]{1,0:T(8,128)(2,1)}, bf16[256,1024]{1,0:T(8,128)(2,1)}, u32[]{:S(2)}, u32[]{:S(2)}) collective-permute-start(bf16[256,1024]{1,0:T(8,128)(2,1)} %collective-permute-done.4), channel_id=1, source_target_pairs={{0,4},{4,8},{8,12},{12,16},{16,20},{20,24},{24,28},{28,0},{1,5},{5... | collective-permute-start | bytes 1572872 | tf_op jit(solution)/shard_map/ppermute | solution.py:64
  114.2 28.3 %copy-start.1 = (bf16[256,1024]{1,0:T(8,128)(2,1)S(1)}, bf16[256,1024]{1,0:T(8,128)(2,1)}, u32[]{:S(2)}) copy-start(bf16[256,1024]{1,0:T(8,128)(2,1)} %param.11) | copy-start | bytes 1572868
  121.6 24.2 %copy-start.5 = (bf16[256,1024]{1,0:T(8,128)(2,1)S(1)}, bf16[256,1024]{1,0:T(8,128)(2,1)}, u32[]{:S(2)}) copy-start(bf16[256,1024]{1,0:T(8,128)(2,1)} %copy-done.4) | copy-start | bytes 1572868
  121.6 24.3 %copy-start.3 = (bf16[256,1024]{1,0:T(8,128)(2,1)S(1)}, bf16[256,1024]{1,0:T(8,128)(2,1)}, u32[]{:S(2)}) copy-start(bf16[256,1024]{1,0:T(8,128)(2,1)} %copy-done.2) | copy-start | bytes 1572868
  121.6 15.4 %collective-permute-start.6 = (bf16[256,1024]{1,0:T(8,128)(2,1)}, bf16[256,1024]{1,0:T(8,128)(2,1)}, u32[]{:S(2)}, u32[]{:S(2)}) collective-permute-start(bf16[256,1024]{1,0:T(8,128)(2,1)} %collective-permute-done.5), channel_id=1, source_target_pairs={{0,4},{4,8},{8,12},{12,16},{16,20},{20,24},{24,28},{28,0},{1,5},{5... | collective-permute-start | bytes 1572872 | tf_op jit(solution)/shard_map/ppermute | solution.py:64
  146.0 3.2 %copy-start.7 = (bf16[4096,1024]{1,0:T(8,128)(2,1)}, bf16[4096,1024]{1,0:T(8,128)(2,1)S(1)}, u32[]{:S(2)}) copy-start(bf16[4096,1024]{1,0:T(8,128)(2,1)S(1)} %constant_dynamic-update-slice_fusion) | copy-start | bytes 25165828
Sparse Core Ops, SparseCore 0:
  10.1 64.1 all-gather.5
  121.7 24.7 all-gather.3
